TPU v7x, 256 devices: a whole 4x4x8 slice. The times are simulated.
256 devices in a mesh: row: 16 (over x, z_lo), col: 16 (over y, z_hi, core).
Axes of the slice: x: 4, y: 4, z: 8 (z_hi: 2, z_lo: 4; z = z_hi * 4 + z_lo), core: 2. Of those that a mesh axis runs over, the one named last changes fastest.
Arguments:
- t2_amps: bfloat16 [16384, 49152], P('row', 'col'), may hold values from -0.5 to 0.5
- l2_amps: bfloat16 [512, 49152], P('row', 'col'), may hold values from -0.02734375 to 0.02734375
Outputs:
- ladder: bfloat16 [512, 49152], P('row', 'col')
All inputs are finite; a program needn't handle non-finite values.
Results may differ from a plain program's by a relative error of at most 0.0044.
Values may be sent and summed in bfloat16 or wider, within the bound.
No kernel may reach another device: no remote copies, remote signals or barrier semaphores. Data moves between devices by JAX's collectives and lax.ppermute only.
A program may use at most 64 MiB of HBM per device.

v0:
```python
import jax
import jax.numpy as jnp
from jax import lax
from jax.sharding import Mesh
from jax.sharding import PartitionSpec as P

ROW = ("row_0", "row_1")
COL = ("col_0", "col_1", "col_2")


def in_blocks(value, dim, size):
    dims = value.shape
    parts = value.reshape(*dims[:dim], size, dims[dim] // size, *dims[dim + 1 :])
    return jnp.moveaxis(parts, dim, 0)


def sum_at_owner(value, axis, dim):
    parts = in_blocks(value, dim, lax.axis_size(axis))
    arrived = lax.all_to_all(parts, axis, split_axis=0, concat_axis=0, tiled=True)
    return arrived.sum(axis=0)


def sum_by_axis(value, axes, dim):
    far, near = axes
    own = sum_at_owner(in_blocks(value, dim, lax.axis_size(far)), near, dim + 1)
    return jnp.sum(lax.all_to_all(own, far, 0, 0, tiled=True), axis=0)


def padded_to(lines, size):
    spare = -lines.shape[0] % size
    if not spare:
        return lines
    return jnp.concatenate([lines, jnp.zeros((spare, *lines.shape[1:]), lines.dtype)])


def from_everyone(value, axis):
    size = lax.axis_size(axis)
    return lax.all_to_all(
        jnp.broadcast_to(value[None], (size, *value.shape)), axis, 0, 0, tiled=True
    )


def in_order(parts, dim):
    dims = list(parts.shape[1:])
    dims[dim] *= parts.shape[0]
    return jnp.moveaxis(parts, 0, dim).reshape(dims)


def gather_axes(value, axes, dim):
    far, near = axes
    initial = from_everyone(value, far)
    parts = jnp.swapaxes(from_everyone(initial, near), 0, 1)
    return in_order(parts.reshape(-1, *value.shape), dim)


def sum_by_parts(value, axes):
    lines = value.reshape(-1, value.shape[-1])
    own = sum_by_axis(padded_to(lines, lax.axis_size(axes[0]) * lax.axis_size(axes[1])), axes, 0)
    whole = gather_axes(own, axes, 0)
    return whole[: len(lines)].reshape(value.shape)


def own_rows(subtotal, axes):
    for axis in axes:
        subtotal = lax.psum_scatter(subtotal, axis, scatter_dimension=0, tiled=True)
    return subtotal


def on_device(t2_amps, l2_amps):
    partial_value = jnp.dot(
        t2_amps,
        lax.all_gather(l2_amps, ROW, axis=0, tiled=True).T,
        preferred_element_type=jnp.float32,
    )
    oooo = sum_by_parts(partial_value, (("col_0", "col_1"), "col_2"))
    oooo_half = oooo.astype(jnp.bfloat16)
    ladder = own_rows(
        lax.dot_general(
            oooo_half, t2_amps, (((0,), (0,)), ((), ())), preferred_element_type=jnp.float32
        ),
        ROW,
    )
    return ladder.astype(jnp.bfloat16)


def solution(mesh):
    finer = Mesh(mesh.devices.reshape(4, 4, 4, 2, 2), ("row_0", "row_1", "col_0", "col_1", "col_2"))
    return jax.shard_map(
        on_device,
        mesh=finer,
        in_specs=(P(ROW, COL), P(ROW, COL)),
        out_specs=P(ROW, COL),
        check_vma=False,
    )
```

profile of v0, /device:TPU:1, one launch (start us, length us, event | category | flops | bytes accessed | tf_op | source)
XLA Modules:
  0.0 296.4 jit_solution(4271393291127959320)
XLA Ops:
  6.5 0.0 all-gather.2.cloned.1.call-start
  6.5 0.7 all-gather.2.cloned.1.call-update
  7.3 0.0 reduce-scatter.3.cloned.1.call-start
  7.3 87.6 %all-gather.2.cloned.1.call-done = bf16[512,3072]{1,0:T(8,128)(2,1)} async-done(((bf16[32,3072]{1,0:T(8,128)(2,1)}), bf16[512,3072]{1,0:T(8,128)(2,1)}) %all-gather.2.cloned.1.call-update) | async-done | bytes 3145744 | tf_op jit(solution)/shard_map/all_gather | solution.py:72
  94.9 6.5 %fusion = f32[1024,512]{1,0:T(8,128)S(1)} fusion(bf16[1024,3072]{1,0:T(8,128)(2,1)} %param.2, bf16[512,3072]{1,0:T(8,128)(2,1)} %all-gather.2.cloned.1.call-done), kind=kOutput, calls=%fused_computation.2 | convolution fusion | flops 3221225472 | bytes 11534336 | tf_op jit(solution)/shard_map/dot_general | solution.py:70
  101.4 0.2 copy.10
  101.7 15.1 %all_to_all.20 = f32[2,8,64,512]{3,2,1,0:T(8,128)S(1)} all-to-all(f32[2,8,64,512]{3,2,1,0:T(8,128)S(1)} %bitcast.11), channel_id=1, replica_groups=mesh['row_0'=4,'row_1'=4,'col_0'=4,'col_1'=2,'col_2'=2] {'col_2'}, dimensions={0} | all-to-all | bytes 4194304 | tf_op jit(solution)/shard_map/all_to_all | solution.py:19
  116.8 0.3 reduce_sum.18
  117.1 33.2 %all_to_all.21 = f32[8,64,512]{2,1,0:T(8,128)S(1)} all-to-all(f32[8,64,512]{2,1,0:T(8,128)S(1)} %reduce_sum.18), channel_id=1, replica_groups=mesh['row_0'=4,'row_1'=4,'col_0'=4,'col_1'=2,'col_2'=2] {'col_0','col_1'}, dimensions={0} | all-to-all | bytes 2097152 | tf_op jit(solution)/shard_map/all_to_all | solution.py:26
  150.3 0.1 reduce_sum.19
  150.5 17.2 %all_to_all.22 = bf16[8,64,512]{2,1,0:T(8,128)(2,1)S(1)} all-to-all(bf16[8,64,512]{2,1,0:T(8,128)(2,1)S(1)} %broadcast_in_dim.4), channel_id=1, replica_groups=mesh['row_0'=4,'row_1'=4,'col_0'=4,'col_1'=2,'col_2'=2] {'col_0','col_1'}, dimensions={0} | all-to-all | bytes 1048576 | tf_op jit(solution)/shard_map/all_to_all | solution.py:38
  167.7 0.1 broadcast_in_dim.5
  167.8 7.5 %all_to_all.23 = bf16[2,8,64,512]{3,2,1,0:T(8,128)(2,1)S(1)} all-to-all(bf16[2,8,64,512]{3,2,1,0:T(8,128)(2,1)S(1)} %broadcast_in_dim.5), channel_id=1, replica_groups=mesh['row_0'=4,'row_1'=4,'col_0'=4,'col_1'=2,'col_2'=2] {'col_2'}, dimensions={0} | all-to-all | bytes 2097152 | tf_op jit(solution)/shard_map/all_to_all | solution.py:38
  175.3 0.1 copy.9
  175.4 8.2 %fusion.1 = f32[512,3072]{1,0:T(8,128)} fusion(bf16[1024,512]{1,0:T(8,128)(2,1)S(1)} %bitcast.12, bf16[1024,3072]{1,0:T(8,128)(2,1)} %param.2), kind=kOutput, calls=%fused_computation.3 | convolution fusion | flops 3221225472 | bytes 13631488 | tf_op jit(solution)/shard_map/dot_general | solution.py:78
  183.6 0.0 reduce-scatter.3.cloned.1.call-update
  183.6 0.0 reduce-scatter.5.cloned.1.call-start
  183.7 61.7 %reduce-scatter.3.cloned.1.call-done = f32[128,3072]{1,0:T(8,128)} async-done(((f32[512,3072]{1,0:T(8,128)}), f32[128,3072]{1,0:T(8,128)}) %reduce-scatter.3.cloned.1.call-update) | async-done | bytes 1572880 | tf_op jit(solution)/shard_map/reduce_scatter | solution.py:65
  245.4 0.0 reduce-scatter.5.cloned.1.call-update
  245.4 42.7 %reduce-scatter.5.cloned.1.call-done = f32[32,3072]{1,0:T(8,128)} async-done(((f32[128,3072]{1,0:T(8,128)}), f32[32,3072]{1,0:T(8,128)}) %reduce-scatter.5.cloned.1.call-update) | async-done | bytes 393232 | tf_op jit(solution)/shard_map/reduce_scatter | solution.py:65
  288.1 1.7 convert_element_type.15
  (1 shorter events, 0.0 us)
Async XLA Ops:
  6.5 88.4 %all-gather.2.cloned.1.call-start = ((), (), s32[]{:S(2)}) async-start(), calls=%async_computation.6 | async-start | bytes 3342336 | tf_op jit(solution)/shard_map/all_gather | solution.py:72
  7.3 238.1 %reduce-scatter.3.cloned.1.call-start = ((), (), s32[]{:S(2)}) async-start(), calls=%async_computation.7 | async-start | bytes 7864320 | tf_op jit(solution)/shard_map/reduce_scatter | solution.py:65
  183.6 104.5 %reduce-scatter.5.cloned.1.call-start = ((), (), s32[]{:S(2)}) async-start(), calls=%async_computation.8 | async-start | bytes 1966080 | tf_op jit(solution)/shard_map/reduce_scatter | solution.py:65
Sparse Core Ops, SparseCore 0:
  9.1 85.7 all-gather.1
  183.7 61.5 reduce-scatter.2
  247.9 40.1 reduce-scatter.4
where the time goes:
time: 297 us; the launch traced here: 296 us
  waiting for transfers between devices  193 us (65%)
  blocking collectives  73.1 us (25%)
  matrix products  14.7 us (5%)
  between operations  13.2 us (4%)
    reduce_scatter x2, waiting for transfers between devices, own_rows(): subtotal = lax.psum_scatter(subtotal, axis, scatter_dimension=0, tiled=True)  104 us
    all_gather x1, waiting for transfers between devices, on_device(): lax.all_gather(l2_amps, ROW, axis=0, tiled=True)  87.6 us
    all_to_all x1, blocking collectives, sum_by_axis(): return jnp.sum(lax.all_to_all(own, far, 0, 0, tiled=True), axis=0)  33.2 us
    all_to_all x2, blocking collectives, from_everyone(): lax.all_to_all(jnp.broadcast_to(value[None], (size, *value.shape)), axis,...  24.8 us
    all_to_all x1, blocking collectives, sum_at_owner(): lax.all_to_all(parts, axis, split_axis=0, concat_axis=0, tiled=True)  15.1 us
    dot_general x1, matrix products, on_device(): lax.dot_general(oooo_half, t2_amps, (((0,), (0,)), ((), ())), preferred_e...  8.19 us
    dot_general x1, matrix products, on_device(): jnp.dot(t2_amps, lax.all_gather(l2_amps, ROW, axis=0, tiled=True).T, pref...  6.51 us
  transfers between devices with their start and end apart: 3, of which 3 were waited for; matrix products, arithmetic and copies ran while one was open for 0% of the time, Pallas kernels for 0%

commit v1 on v0

--- a/solution.py
+++ b/solution.py
@@ -67,11 +67,14 @@
 
 
 def on_device(t2_amps, l2_amps):
-    partial_value = jnp.dot(
-        t2_amps,
-        lax.all_gather(l2_amps, ROW, axis=0, tiled=True).T,
-        preferred_element_type=jnp.float32,
-    )
+
+    def load_slot(field):
+        top = jnp.stack([field for _ in range(jax.lax.axis_size(ROW))], axis=0)
+        arr_now = jax.lax.all_to_all(top, axis_name=ROW, split_axis=0, concat_axis=0)
+        low = jnp.concatenate(arr_now, 0)
+        return low
+
+    partial_value = jnp.dot(t2_amps, load_slot(l2_amps).T, preferred_element_type=jnp.float32)
     oooo = sum_by_parts(partial_value, (("col_0", "col_1"), "col_2"))
     oooo_half = oooo.astype(jnp.bfloat16)
     ladder = own_rows(

time: 297 us -> 282 us (0.949)
  waiting for transfers between devices: 193 us -> 104 us
  blocking collectives: 73.1 us -> 148 us
  matrix products: 14.7 us -> 11.6 us
    all_gather x1 -> x0, waiting for transfers between devices: 87.6 us -> none  [on_device(): lax.all_gather(l2_amps, ROW, axis=0, tiled=True)]
    all_to_all x0 -> x1, blocking collectives: none -> 81 us  [load_slot(): jax.lax.all_to_all(top, axis_name=ROW, split_axis=0, concat_axis=0)]
    all_to_all x1, blocking collectives: 15.1 us -> 6.73 us  [sum_at_owner(): lax.all_to_all(parts, axis, split_axis=0, concat_axis=0, tiled=True)]
    dot_general x1, matrix products: 6.51 us -> 3.44 us  [on_device(): jnp.dot(t2_amps, load_slot(l2_amps).T, preferred_element_type=jnp.float32)]
  transfers between devices with their start and end apart: 3 -> 2, of which waited for: 3 -> 2; matrix products, arithmetic and copies ran while one was open for 0% -> 0% of each run, Pallas kernels for 0% -> 0%
where the time goes in v1:
time: 282 us; the launch traced here: 281 us
  blocking collectives  148 us (52%)
  waiting for transfers between devices  104 us (37%)
  between operations  13.5 us (5%)
  matrix products  11.6 us (4%)
    reduce_scatter x2, waiting for transfers between devices, own_rows(): subtotal = lax.psum_scatter(subtotal, axis, scatter_dimension=0, tiled=True)  104 us
    all_to_all x1, blocking collectives, load_slot(): jax.lax.all_to_all(top, axis_name=ROW, split_axis=0, concat_axis=0)  81 us
    all_to_all x1, blocking collectives, sum_by_axis(): return jnp.sum(lax.all_to_all(own, far, 0, 0, tiled=True), axis=0)  35.7 us
    all_to_all x2, blocking collectives, from_everyone(): lax.all_to_all(jnp.broadcast_to(value[None], (size, *value.shape)), axis,...  24.8 us
    dot_general x1, matrix products, on_device(): lax.dot_general(oooo_half, t2_amps, (((0,), (0,)), ((), ())), preferred_e...  8.19 us
    all_to_all x1, blocking collectives, sum_at_owner(): lax.all_to_all(parts, axis, split_axis=0, concat_axis=0, tiled=True)  6.73 us
  transfers between devices with their start and end apart: 2, of which 2 were waited for; matrix products, arithmetic and copies ran while one was open for 0% of the time, Pallas kernels for 0%

profile of v1, /device:TPU:1, one launch (start us, length us, event | category | flops | bytes accessed | tf_op | source)
XLA Modules:
  0.0 281.2 jit_solution(8237848987299480635)
XLA Ops:
  6.5 0.0 reduce-scatter.3.cloned.1.call-start
  6.5 1.3 stack.2
  7.8 0.0 copy-start
  7.9 81.0 %all_to_all.25 = bf16[16,32,3072]{2,1,0:T(8,128)(2,1)S(1)} all-to-all(bf16[16,32,3072]{2,1,0:T(8,128)(2,1)S(1)} %stack.2), channel_id=1, replica_groups=mesh['row_0'=4,'row_1'=4,'col_0'=4,'col_1'=2,'col_2'=2] {'row_0','row_1'}, dimensions={0} | all-to-all | bytes 6291456 | tf_op jit(solution)/shard_map/all_to_all | solution.py:73
  88.9 0.0 copy-done
  88.9 3.4 %convolution_bitcast_fusion = f32[2,8,64,512]{3,2,0,1:T(8,128)S(1)} fusion(bf16[8,2,64,3072]{3,2,1,0:T(8,128)(2,1)S(1)} %bitcast.15, bf16[512,3072,1,1]{1,0,3,2:T(8,128)(2,1)S(1)} %bitcast.17), kind=kOutput, calls=%fused_computation.1 | convolution fusion | flops 3221225472 | bytes 11534336 | tf_op jit(solution)/shard_map/dot_general | solution.py:77
  92.3 0.2 copy.5
  92.5 6.7 %all_to_all.26 = f32[2,8,64,512]{3,2,1,0:T(8,128)S(1)} all-to-all(f32[2,8,64,512]{3,2,1,0:T(8,128)S(1)} %copy.5), channel_id=1, replica_groups=mesh['row_0'=4,'row_1'=4,'col_0'=4,'col_1'=2,'col_2'=2] {'col_2'}, dimensions={0} | all-to-all | bytes 4194304 | tf_op jit(solution)/shard_map/all_to_all | solution.py:19
  99.3 0.3 reduce_sum.18
  99.6 35.7 %all_to_all.27 = f32[8,64,512]{2,1,0:T(8,128)S(1)} all-to-all(f32[8,64,512]{2,1,0:T(8,128)S(1)} %reduce_sum.18), channel_id=1, replica_groups=mesh['row_0'=4,'row_1'=4,'col_0'=4,'col_1'=2,'col_2'=2] {'col_0','col_1'}, dimensions={0} | all-to-all | bytes 2097152 | tf_op jit(solution)/shard_map/all_to_all | solution.py:26
  135.2 0.1 reduce_sum.19
  135.3 18.8 %all_to_all.28 = bf16[8,64,512]{2,1,0:T(8,128)(2,1)S(1)} all-to-all(bf16[8,64,512]{2,1,0:T(8,128)(2,1)S(1)} %broadcast_in_dim.4), channel_id=1, replica_groups=mesh['row_0'=4,'row_1'=4,'col_0'=4,'col_1'=2,'col_2'=2] {'col_0','col_1'}, dimensions={0} | all-to-all | bytes 1048576 | tf_op jit(solution)/shard_map/all_to_all | solution.py:38
  154.2 0.1 broadcast_in_dim.5
  154.3 6.0 %all_to_all.29 = bf16[2,8,64,512]{3,2,1,0:T(8,128)(2,1)S(1)} all-to-all(bf16[2,8,64,512]{3,2,1,0:T(8,128)(2,1)S(1)} %broadcast_in_dim.5), channel_id=1, replica_groups=mesh['row_0'=4,'row_1'=4,'col_0'=4,'col_1'=2,'col_2'=2] {'col_2'}, dimensions={0} | all-to-all | bytes 2097152 | tf_op jit(solution)/shard_map/all_to_all | solution.py:38
  160.3 0.1 copy.9
  160.4 8.2 %fusion = f32[512,3072]{1,0:T(8,128)} fusion(bf16[1024,512]{1,0:T(8,128)(2,1)S(1)} %bitcast.16, bf16[1024,3072]{1,0:T(8,128)(2,1)} %param.2), kind=kOutput, calls=%fused_computation.2 | convolution fusion | flops 3221225472 | bytes 13631488 | tf_op jit(solution)/shard_map/dot_general | solution.py:81
  168.5 0.0 reduce-scatter.3.cloned.1.call-update
  168.6 0.0 reduce-scatter.5.cloned.1.call-start
  168.6 61.3 %reduce-scatter.3.cloned.1.call-done = f32[128,3072]{1,0:T(8,128)} async-done(((f32[512,3072]{1,0:T(8,128)}), f32[128,3072]{1,0:T(8,128)}) %reduce-scatter.3.cloned.1.call-update) | async-done | bytes 1572880 | tf_op jit(solution)/shard_map/reduce_scatter | solution.py:65
  230.0 0.0 reduce-scatter.5.cloned.1.call-update
  230.0 42.7 %reduce-scatter.5.cloned.1.call-done = f32[32,3072]{1,0:T(8,128)} async-done(((f32[128,3072]{1,0:T(8,128)}), f32[32,3072]{1,0:T(8,128)}) %reduce-scatter.5.cloned.1.call-update) | async-done | bytes 393232 | tf_op jit(solution)/shard_map/reduce_scatter | solution.py:65
  272.7 1.7 convert_element_type.15
  (1 shorter events, 0.0 us)
Async XLA Ops:
  6.5 223.4 %reduce-scatter.3.cloned.1.call-start = ((), (), s32[]{:S(2)}) async-start(), calls=%async_computation.7 | async-start | bytes 7864320 | tf_op jit(solution)/shard_map/reduce_scatter | solution.py:65
  7.8 81.0 %copy-start = (bf16[1024,3072]{1,0:T(8,128)(2,1)S(1)}, bf16[1024,3072]{1,0:T(8,128)(2,1)}, u32[]{:S(2)}) copy-start(bf16[1024,3072]{1,0:T(8,128)(2,1)} %param.2) | copy-start | bytes 18874372
  168.6 104.1 %reduce-scatter.5.cloned.1.call-start = ((), (), s32[]{:S(2)}) async-start(), calls=%async_computation.8 | async-start | bytes 1966080 | tf_op jit(solution)/shard_map/reduce_scatter | solution.py:65
Sparse Core Ops, SparseCore 0:
  168.7 61.2 reduce-scatter.2
  232.5 40.1 reduce-scatter.4
